TPU v7x, 32 devices: a whole 2x2x4 slice. The times are simulated.
32 devices in a mesh: blk: 32 (over z, y, x, core).
Axes of the slice: x: 2, y: 2, z: 4, core: 2. Of those that a mesh axis runs over, the one named last changes fastest.
Arguments:
- samples: bfloat16 [8192, 2048], P('blk'), may hold values from -6 to 6
- hubs: int32 [64], replicated, may hold values from 0 to 8191, as said below
- start: int32 [1], replicated, may hold values from 1 to 13
Outputs:
- self_stat: float32 [8192, 256], P('blk')
- ahead_stat: float32 [3, 8192, 256], P(None, 'blk')
- behind_stat: float32 [3, 8192, 256], P(None, 'blk')
Inputs may be any that keep to these rules, and one draw needn't show every extreme that they name: `hubs`: the 64 indices are distinct.
All inputs are finite; a program needn't handle non-finite values.
Results may differ from a plain program's by a relative error of at most 0.0049.
Values may be sent and summed in bfloat16 or wider, within the bound.
No kernel may reach another device: no remote copies, remote signals or barrier semaphores. Data moves between devices by JAX's collectives and lax.ppermute only.
A program may use at most 64 MiB of HBM per device.

v0:
```python
import math

import jax
import jax.numpy as jnp
from jax import lax
from jax.sharding import PartitionSpec as P


def shifted(block, axis, distance):
    devices = range(lax.axis_size(axis))
    route = [((i - distance) % len(devices), i) for i in devices]
    return lax.ppermute(block, axis, route)


def row_scale(resid):
    wide = resid.astype(jnp.float32)
    return 1.0 / jnp.sqrt(jnp.maximum(jnp.sum(wide * wide, axis=1), 1.0))


def correlate(resid, scale, partner):
    dots = lax.dot_general(
        resid, partner, (((1,), (1,)), ((), ())), preferred_element_type=jnp.float32
    )
    return (dots * scale[:, None] * row_scale(partner)[None, :]).astype(jnp.bfloat16)


def to_stat(rounded, factor):
    values = lax.optimization_barrier(rounded).astype(jnp.float32)
    return factor * (0.5 * (jnp.log1p(values) - jnp.log1p(-values)))


def shards(samples, hubs, start):
    rows = samples.shape[0]
    width = samples.shape[1]
    factor = math.sqrt(width - hubs.shape[0] - 3)
    count = lax.axis_size("blk")
    mine = lax.axis_index("blk")
    levels = count.bit_length() - 2
    offset = start[0]
    owner = hubs // rows
    within = hubs % rows
    picker = jnp.logical_and(
        (owner == mine)[:, None], within[:, None] == jnp.arange(rows, dtype=jnp.int32)[None, :]
    ).astype(jnp.bfloat16)
    hub_rows = lax.psum(jnp.dot(picker, samples, preferred_element_type=jnp.float32), "blk")
    gram = jnp.dot(hub_rows, hub_rows.T, precision=lax.Precision.HIGHEST)
    proj = jnp.dot(samples, hub_rows.astype(jnp.bfloat16).T, preferred_element_type=jnp.float32)
    factor_lower = jnp.linalg.cholesky(gram)
    coef = jax.scipy.linalg.cho_solve((factor_lower, True), proj.T).T
    resid = (
        samples.astype(jnp.float32) - jnp.dot(coef, hub_rows, precision=lax.Precision.HIGHEST)
    ).astype(jnp.bfloat16)
    scale = row_scale(resid)
    own = correlate(resid, scale, resid)
    diag = jnp.arange(rows)[:, None] == jnp.arange(rows)[None, :]
    own_stat = jnp.where(diag, 0.0, to_stat(own, factor))
    partner = resid
    for level in range(levels):
        moved = shifted(partner, "blk", -(1 << level))
        partner = jnp.where(offset >> level & 1 == 1, moved, partner)
    ahead = []
    turned = []
    for index in range(3):
        if index > 0:
            partner = shifted(partner, "blk", -1)
        tile = correlate(resid, scale, partner)
        ahead.append(to_stat(tile, factor))
        turned.append(tile.T)
    returned = []
    for index in range(3):
        tile = turned[index]
        for extra in range(index):
            tile = shifted(tile, "blk", 1)
        for level in range(levels):
            moved = shifted(tile, "blk", 1 << level)
            tile = jnp.where(offset >> level & 1 == 1, moved, tile)
        returned.append(tile)
    behind = jnp.stack([to_stat(tile, factor) for tile in returned])
    return (own_stat, jnp.stack(ahead), behind)


def solution(mesh):
    in_specs = (P("blk", None), P(), P())
    out_specs = (P("blk", None), P(None, "blk", None), P(None, "blk", None))
    return jax.shard_map(shards, mesh=mesh, in_specs=in_specs, out_specs=out_specs, check_vma=False)
```

profile of v0, /device:TPU:0, one launch (start us, length us, event | category | flops | bytes accessed | tf_op | source)
XLA Modules:
  0.0 362.8 jit_solution(15652582608777804637)
XLA Ops:
  8.5 2.4 fusion.40
  10.9 134.7 %all-reduce.2.cloned.1.call-done = f32[64,2048]{1,0:T(8,128)} async-done(((f32[64,2048]{1,0:T(8,128)}), f32[64,2048]{1,0:T(8,128)}) %all-reduce.2.cloned.1.call-update) | async-done | bytes 524304 | tf_op jit(solution)/shard_map/psum | solution.py:45
  147.6 5.8 %cholesky.16 = f32[64,64]{1,0:T(8,128)S(1)} custom-call(f32[64,64]{1,0:T(8,128)S(1)} %fusion.47), custom_call_target="Cholesky" | custom-call | tf_op jit(solution)/shard_map/jit(cholesky)/cholesky | solution.py:48
  154.7 4.9 %custom-call.10 = f32[1,64,64]{1,2,0:T(8,128)S(1)} custom-call(f32[1,64,64]{2,1,0:T(8,128)S(1)} %fusion.42), custom_call_target="InvertDiagBlocksLowerTriangular" | custom-call | tf_op jit(solution)/shard_map/jit(_cho_solve)/triangular_solve | solution.py:49
  160.6 2.1 multiply_reduce_fusion.3
  165.2 11.7 %collective-permute-done = bf16[256,2048]{1,0:T(8,128)(2,1)S(1)} collective-permute-done((bf16[256,2048]{1,0:T(8,128)(2,1)S(1)}, bf16[256,2048]{1,0:T(8,128)(2,1)S(1)}, u32[]{:S(2)}, u32[]{:S(2)}) %collective-permute-start) | collective-permute-done | bytes 1048608 | tf_op jit(solution)/shard_map/ppermute | solution.py:12
  178.4 23.6 %collective-permute-done.1 = bf16[256,2048]{1,0:T(8,128)(2,1)S(1)} collective-permute-done((bf16[256,2048]{1,0:T(8,128)(2,1)S(1)}, bf16[256,2048]{1,0:T(8,128)(2,1)S(1)}, u32[]{:S(2)}, u32[]{:S(2)}) %collective-permute-start.1) | collective-permute-done | bytes 1048608 | tf_op jit(solution)/shard_map/ppermute | solution.py:12
  202.9 24.4 %collective-permute-done.2 = bf16[256,2048]{1,0:T(8,128)(2,1)S(1)} collective-permute-done((bf16[256,2048]{1,0:T(8,128)(2,1)S(1)}, bf16[256,2048]{1,0:T(8,128)(2,1)S(1)}, u32[]{:S(2)}, u32[]{:S(2)}) %collective-permute-start.2) | collective-permute-done | bytes 1048608 | tf_op jit(solution)/shard_map/ppermute | solution.py:12
  229.0 22.8 %collective-permute-done.3 = bf16[256,2048]{1,0:T(8,128)(2,1)S(1)} collective-permute-done((bf16[256,2048]{1,0:T(8,128)(2,1)S(1)}, bf16[256,2048]{1,0:T(8,128)(2,1)S(1)}, u32[]{:S(2)}, u32[]{:S(2)}) %collective-permute-start.3) | collective-permute-done | bytes 1048608 | tf_op jit(solution)/shard_map/ppermute | solution.py:12
  252.3 6.7 %collective-permute-start.4 = (bf16[256,2048]{1,0:T(8,128)(2,1)S(1)}, bf16[256,2048]{1,0:T(8,128)(2,1)S(1)}, u32[]{:S(2)}, u32[]{:S(2)}) collective-permute-start(bf16[256,2048]{1,0:T(8,128)(2,1)S(1)} %get-tuple-element.7), channel_id=1, source_target_pairs={{1,0},{2,1},{3,2},{4,3},{5,4},{6,5},{7,6},{8,7},{9,8},{10,9},{11,1... | collective-permute-start | bytes 3145736 | tf_op jit(solution)/shard_map/ppermute | solution.py:12
  260.0 7.6 %collective-permute-done.6 = bf16[256,256]{1,0:T(8,128)(2,1)S(1)} collective-permute-done((bf16[256,256]{1,0:T(8,128)(2,1)S(1)}, bf16[256,256]{1,0:T(8,128)(2,1)S(1)}, u32[]{:S(2)}, u32[]{:S(2)}) %collective-permute-start.6) | collective-permute-done | bytes 131104 | tf_op jit(solution)/shard_map/ppermute | solution.py:12
  268.6 7.6 %collective-permute-done.7 = bf16[256,256]{1,0:T(8,128)(2,1)S(1)} collective-permute-done((bf16[256,256]{1,0:T(8,128)(2,1)S(1)}, bf16[256,256]{1,0:T(8,128)(2,1)S(1)}, u32[]{:S(2)}, u32[]{:S(2)}) %collective-permute-start.7) | collective-permute-done | bytes 131104 | tf_op jit(solution)/shard_map/ppermute | solution.py:12
  277.3 5.3 %collective-permute-start.5 = (bf16[256,2048]{1,0:T(8,128)(2,1)S(1)}, bf16[256,2048]{1,0:T(8,128)(2,1)S(1)}, u32[]{:S(2)}, u32[]{:S(2)}) collective-permute-start(bf16[256,2048]{1,0:T(8,128)(2,1)S(1)} %collective-permute-done.4), channel_id=1, source_target_pairs={{1,0},{2,1},{3,2},{4,3},{5,4},{6,5},{7,6},{8,7},{9,8},{10,9},{11,1... | collective-permute-start | bytes 3145736 | tf_op jit(solution)/shard_map/ppermute | solution.py:12
  282.8 2.6 collective-permute-done.10
  285.5 8.0 %collective-permute-done.11 = bf16[256,256]{1,0:T(8,128)(2,1)S(1)} collective-permute-done((bf16[256,256]{1,0:T(8,128)(2,1)S(1)}, bf16[256,256]{1,0:T(8,128)(2,1)S(1)}, u32[]{:S(2)}, u32[]{:S(2)}) %collective-permute-start.11) | collective-permute-done | bytes 131104 | tf_op jit(solution)/shard_map/ppermute | solution.py:12
  293.5 4.7 %collective-permute-done.9 = bf16[256,256]{1,0:T(8,128)(2,1)S(1)} collective-permute-done((bf16[256,256]{1,0:T(8,128)(2,1)S(1)}, bf16[256,256]{1,0:T(8,128)(2,1)S(1)}, u32[]{:S(2)}, u32[]{:S(2)}) %collective-permute-start.9) | collective-permute-done | bytes 131104 | tf_op jit(solution)/shard_map/ppermute | solution.py:12
  298.3 5.6 %collective-permute-done.12 = bf16[256,256]{1,0:T(8,128)(2,1)S(1)} collective-permute-done((bf16[256,256]{1,0:T(8,128)(2,1)S(1)}, bf16[256,256]{1,0:T(8,128)(2,1)S(1)}, u32[]{:S(2)}, u32[]{:S(2)}) %collective-permute-start.12) | collective-permute-done | bytes 131104 | tf_op jit(solution)/shard_map/ppermute | solution.py:12
  304.9 6.8 %collective-permute-done.13 = bf16[256,256]{1,0:T(8,128)(2,1)S(1)} collective-permute-done((bf16[256,256]{1,0:T(8,128)(2,1)S(1)}, bf16[256,256]{1,0:T(8,128)(2,1)S(1)}, u32[]{:S(2)}, u32[]{:S(2)}) %collective-permute-start.13) | collective-permute-done | bytes 131104 | tf_op jit(solution)/shard_map/ppermute | solution.py:12
  311.7 2.5 collective-permute-done.15
  314.4 7.8 %collective-permute-done.16 = bf16[256,256]{1,0:T(8,128)(2,1)S(1)} collective-permute-done((bf16[256,256]{1,0:T(8,128)(2,1)S(1)}, bf16[256,256]{1,0:T(8,128)(2,1)S(1)}, u32[]{:S(2)}, u32[]{:S(2)}) %collective-permute-start.16) | collective-permute-done | bytes 131104 | tf_op jit(solution)/shard_map/ppermute | solution.py:12
  322.3 8.0 %collective-permute-done.17 = bf16[256,256]{1,0:T(8,128)(2,1)S(1)} collective-permute-done((bf16[256,256]{1,0:T(8,128)(2,1)S(1)}, bf16[256,256]{1,0:T(8,128)(2,1)S(1)}, u32[]{:S(2)}, u32[]{:S(2)}) %collective-permute-start.17) | collective-permute-done | bytes 131104 | tf_op jit(solution)/shard_map/ppermute | solution.py:12
  330.7 9.5 %collective-permute-done.18 = bf16[256,256]{1,0:T(8,128)(2,1)S(1)} collective-permute-done((bf16[256,256]{1,0:T(8,128)(2,1)S(1)}, bf16[256,256]{1,0:T(8,128)(2,1)S(1)}, u32[]{:S(2)}, u32[]{:S(2)}) %collective-permute-start.18) | collective-permute-done | bytes 131104 | tf_op jit(solution)/shard_map/ppermute | solution.py:12
  340.5 7.5 %collective-permute-done.19 = bf16[256,256]{1,0:T(8,128)(2,1)S(1)} collective-permute-done((bf16[256,256]{1,0:T(8,128)(2,1)S(1)}, bf16[256,256]{1,0:T(8,128)(2,1)S(1)}, u32[]{:S(2)}, u32[]{:S(2)}) %collective-permute-start.19) | collective-permute-done | bytes 131104 | tf_op jit(solution)/shard_map/ppermute | solution.py:12
  349.3 5.5 %collective-permute-done.20 = bf16[256,256]{1,0:T(8,128)(2,1)S(1)} collective-permute-done((bf16[256,256]{1,0:T(8,128)(2,1)S(1)}, bf16[256,256]{1,0:T(8,128)(2,1)S(1)}, u32[]{:S(2)}, u32[]{:S(2)}) %collective-permute-start.20) | collective-permute-done | bytes 131104 | tf_op jit(solution)/shard_map/ppermute | solution.py:12
  (75 shorter events, 19.8 us)
Async XLA Ops:
  7.2 138.5 %all-reduce.2.cloned.1.call-start = ((), (), s32[]{:S(2)}) async-start(), calls=%async_computation | async-start | bytes 1048576 | tf_op jit(solution)/shard_map/psum | solution.py:45
  10.9 148.7 %copy-start = (bf16[256,2048]{1,0:T(8,128)(2,1)S(1)}, bf16[256,2048]{1,0:T(8,128)(2,1)}, u32[]{:S(2)}) copy-start(bf16[256,2048]{1,0:T(8,128)(2,1)} %param.3) | copy-start | bytes 3145732
  145.6 14.0 %copy-start.1 = (f32[64,2048]{1,0:T(8,128)S(1)}, f32[64,2048]{1,0:T(8,128)}, u32[]{:S(2)}) copy-start(f32[64,2048]{1,0:T(8,128)} %all-reduce.2.cloned.1.call-done) | copy-start | bytes 1572868
  162.6 14.2 %collective-permute-start = (bf16[256,2048]{1,0:T(8,128)(2,1)S(1)}, bf16[256,2048]{1,0:T(8,128)(2,1)S(1)}, u32[]{:S(2)}, u32[]{:S(2)}) collective-permute-start(bf16[256,2048]{1,0:T(8,128)(2,1)S(1)} %get-tuple-element.9), channel_id=1, source_target_pairs={{1,0},{2,1},{3,2},{4,3},{5,4},{6,5},{7,6},{8,7},{9,8},{10,9},{11,1... | collective-permute-start | bytes 3145736 | tf_op jit(solution)/shard_map/ppermute | solution.py:12
  177.0 25.0 %collective-permute-start.1 = (bf16[256,2048]{1,0:T(8,128)(2,1)S(1)}, bf16[256,2048]{1,0:T(8,128)(2,1)S(1)}, u32[]{:S(2)}, u32[]{:S(2)}) collective-permute-start(bf16[256,2048]{1,0:T(8,128)(2,1)S(1)} %broadcast_select_fusion), channel_id=1, source_target_pairs={{2,0},{3,1},{4,2},{5,3},{6,4},{7,5},{8,6},{9,7},{10,8},{11,9},{12,... | collective-permute-start | bytes 3145736 | tf_op jit(solution)/shard_map/ppermute | solution.py:12
  202.1 25.2 %collective-permute-start.2 = (bf16[256,2048]{1,0:T(8,128)(2,1)S(1)}, bf16[256,2048]{1,0:T(8,128)(2,1)S(1)}, u32[]{:S(2)}, u32[]{:S(2)}) collective-permute-start(bf16[256,2048]{1,0:T(8,128)(2,1)S(1)} %broadcast_select_fusion.1), channel_id=1, source_target_pairs={{4,0},{5,1},{6,2},{7,3},{8,4},{9,5},{10,6},{11,7},{12,8},{13,9},{1... | collective-permute-start | bytes 3145736 | tf_op jit(solution)/shard_map/ppermute | solution.py:12
  227.4 24.4 %collective-permute-start.3 = (bf16[256,2048]{1,0:T(8,128)(2,1)S(1)}, bf16[256,2048]{1,0:T(8,128)(2,1)S(1)}, u32[]{:S(2)}, u32[]{:S(2)}) collective-permute-start(bf16[256,2048]{1,0:T(8,128)(2,1)S(1)} %broadcast_select_fusion.2), channel_id=1, source_target_pairs={{8,0},{9,1},{10,2},{11,3},{12,4},{13,5},{14,6},{15,7},{16,8},{17,9... | collective-permute-start | bytes 3145736 | tf_op jit(solution)/shard_map/ppermute | solution.py:12
  252.3 24.0 %collective-permute-start.4 = (bf16[256,2048]{1,0:T(8,128)(2,1)S(1)}, bf16[256,2048]{1,0:T(8,128)(2,1)S(1)}, u32[]{:S(2)}, u32[]{:S(2)}) collective-permute-start(bf16[256,2048]{1,0:T(8,128)(2,1)S(1)} %get-tuple-element.7), channel_id=1, source_target_pairs={{1,0},{2,1},{3,2},{4,3},{5,4},{6,5},{7,6},{8,7},{9,8},{10,9},{11,1... | collective-permute-start | bytes 3145736 | tf_op jit(solution)/shard_map/ppermute | solution.py:12
  259.4 8.1 %collective-permute-start.6 = (bf16[256,256]{1,0:T(8,128)(2,1)S(1)}, bf16[256,256]{1,0:T(8,128)(2,1)S(1)}, u32[]{:S(2)}, u32[]{:S(2)}) collective-permute-start(bf16[256,256]{1,0:T(8,128)(2,1)S(1)} %bitcast.47), channel_id=1, source_target_pairs={{31,0},{0,1},{1,2},{2,3},{3,4},{4,5},{5,6},{6,7},{7,8},{8,9},{9,10... | collective-permute-start | bytes 393224 | tf_op jit(solution)/shard_map/ppermute | solution.py:12
  267.6 8.6 %collective-permute-start.7 = (bf16[256,256]{1,0:T(8,128)(2,1)S(1)}, bf16[256,256]{1,0:T(8,128)(2,1)S(1)}, u32[]{:S(2)}, u32[]{:S(2)}) collective-permute-start(bf16[256,256]{1,0:T(8,128)(2,1)S(1)} %broadcast_select_fusion.6), channel_id=1, source_target_pairs={{30,0},{31,1},{0,2},{1,3},{2,4},{3,5},{4,6},{5,7},{6,8},{7,9},{8,1... | collective-permute-start | bytes 393224 | tf_op jit(solution)/shard_map/ppermute | solution.py:12
  276.3 9.1 %collective-permute-start.8 = (bf16[256,256]{1,0:T(8,128)(2,1)S(1)}, bf16[256,256]{1,0:T(8,128)(2,1)S(1)}, u32[]{:S(2)}, u32[]{:S(2)}) collective-permute-start(bf16[256,256]{1,0:T(8,128)(2,1)S(1)} %broadcast_select_fusion.9), channel_id=1, source_target_pairs={{28,0},{29,1},{30,2},{31,3},{0,4},{1,5},{2,6},{3,7},{4,8},{5,9},{6... | collective-permute-start | bytes 393224 | tf_op jit(solution)/shard_map/ppermute | solution.py:12
  277.2 8.2 %collective-permute-start.10 = (bf16[256,256]{1,0:T(8,128)(2,1)S(1)}, bf16[256,256]{1,0:T(8,128)(2,1)S(1)}, u32[]{:S(2)}, u32[]{:S(2)}) collective-permute-start(bf16[256,256]{1,0:T(8,128)(2,1)S(1)} %bitcast.48), channel_id=1, source_target_pairs={{31,0},{0,1},{1,2},{2,3},{3,4},{4,5},{5,6},{6,7},{7,8},{8,9},{9,10... | collective-permute-start | bytes 393224 | tf_op jit(solution)/shard_map/ppermute | solution.py:12
  277.3 26.7 %collective-permute-start.5 = (bf16[256,2048]{1,0:T(8,128)(2,1)S(1)}, bf16[256,2048]{1,0:T(8,128)(2,1)S(1)}, u32[]{:S(2)}, u32[]{:S(2)}) collective-permute-start(bf16[256,2048]{1,0:T(8,128)(2,1)S(1)} %collective-permute-done.4), channel_id=1, source_target_pairs={{1,0},{2,1},{3,2},{4,3},{5,4},{6,5},{7,6},{8,7},{9,8},{10,9},{11,1... | collective-permute-start | bytes 3145736 | tf_op jit(solution)/shard_map/ppermute | solution.py:12
  285.4 8.1 %collective-permute-start.11 = (bf16[256,256]{1,0:T(8,128)(2,1)S(1)}, bf16[256,256]{1,0:T(8,128)(2,1)S(1)}, u32[]{:S(2)}, u32[]{:S(2)}) collective-permute-start(bf16[256,256]{1,0:T(8,128)(2,1)S(1)} %collective-permute-done.10), channel_id=1, source_target_pairs={{31,0},{0,1},{1,2},{2,3},{3,4},{4,5},{5,6},{6,7},{7,8},{8,9},{9,10... | collective-permute-start | bytes 393224 | tf_op jit(solution)/shard_map/ppermute | solution.py:12
  285.4 12.9 %collective-permute-start.9 = (bf16[256,256]{1,0:T(8,128)(2,1)S(1)}, bf16[256,256]{1,0:T(8,128)(2,1)S(1)}, u32[]{:S(2)}, u32[]{:S(2)}) collective-permute-start(bf16[256,256]{1,0:T(8,128)(2,1)S(1)} %broadcast_select_fusion.12), channel_id=1, source_target_pairs={{24,0},{25,1},{26,2},{27,3},{28,4},{29,5},{30,6},{31,7},{0,8},{1,9... | collective-permute-start | bytes 393224 | tf_op jit(solution)/shard_map/ppermute | solution.py:12
  293.5 10.4 %collective-permute-start.12 = (bf16[256,256]{1,0:T(8,128)(2,1)S(1)}, bf16[256,256]{1,0:T(8,128)(2,1)S(1)}, u32[]{:S(2)}, u32[]{:S(2)}) collective-permute-start(bf16[256,256]{1,0:T(8,128)(2,1)S(1)} %broadcast_select_fusion.5), channel_id=1, source_target_pairs={{30,0},{31,1},{0,2},{1,3},{2,4},{3,5},{4,6},{5,7},{6,8},{7,9},{8,1... | collective-permute-start | bytes 393224 | tf_op jit(solution)/shard_map/ppermute | solution.py:12
  303.9 7.8 %collective-permute-start.13 = (bf16[256,256]{1,0:T(8,128)(2,1)S(1)}, bf16[256,256]{1,0:T(8,128)(2,1)S(1)}, u32[]{:S(2)}, u32[]{:S(2)}) collective-permute-start(bf16[256,256]{1,0:T(8,128)(2,1)S(1)} %broadcast_select_fusion.8), channel_id=1, source_target_pairs={{28,0},{29,1},{30,2},{31,3},{0,4},{1,5},{2,6},{3,7},{4,8},{5,9},{6... | collective-permute-start | bytes 393224 | tf_op jit(solution)/shard_map/ppermute | solution.py:12
  304.8 9.4 %collective-permute-start.15 = (bf16[256,256]{1,0:T(8,128)(2,1)S(1)}, bf16[256,256]{1,0:T(8,128)(2,1)S(1)}, u32[]{:S(2)}, u32[]{:S(2)}) collective-permute-start(bf16[256,256]{1,0:T(8,128)(2,1)S(1)} %bitcast.49), channel_id=1, source_target_pairs={{31,0},{0,1},{1,2},{2,3},{3,4},{4,5},{5,6},{6,7},{7,8},{8,9},{9,10... | collective-permute-start | bytes 393224 | tf_op jit(solution)/shard_map/ppermute | solution.py:12
  311.7 10.6 %collective-permute-start.14 = (bf16[256,256]{1,0:T(8,128)(2,1)S(1)}, bf16[256,256]{1,0:T(8,128)(2,1)S(1)}, u32[]{:S(2)}, u32[]{:S(2)}) collective-permute-start(bf16[256,256]{1,0:T(8,128)(2,1)S(1)} %broadcast_select_fusion.11), channel_id=1, source_target_pairs={{24,0},{25,1},{26,2},{27,3},{28,4},{29,5},{30,6},{31,7},{0,8},{1,9... | collective-permute-start | bytes 393224 | tf_op jit(solution)/shard_map/ppermute | solution.py:12
  314.2 8.0 %collective-permute-start.16 = (bf16[256,256]{1,0:T(8,128)(2,1)S(1)}, bf16[256,256]{1,0:T(8,128)(2,1)S(1)}, u32[]{:S(2)}, u32[]{:S(2)}) collective-permute-start(bf16[256,256]{1,0:T(8,128)(2,1)S(1)} %collective-permute-done.15), channel_id=1, source_target_pairs={{31,0},{0,1},{1,2},{2,3},{3,4},{4,5},{5,6},{6,7},{7,8},{8,9},{9,10... | collective-permute-start | bytes 393224 | tf_op jit(solution)/shard_map/ppermute | solution.py:12
  322.2 8.0 %collective-permute-start.17 = (bf16[256,256]{1,0:T(8,128)(2,1)S(1)}, bf16[256,256]{1,0:T(8,128)(2,1)S(1)}, u32[]{:S(2)}, u32[]{:S(2)}) collective-permute-start(bf16[256,256]{1,0:T(8,128)(2,1)S(1)} %collective-permute-done.16), channel_id=1, source_target_pairs={{31,0},{0,1},{1,2},{2,3},{3,4},{4,5},{5,6},{6,7},{7,8},{8,9},{9,10... | collective-permute-start | bytes 393224 | tf_op jit(solution)/shard_map/ppermute | solution.py:12
  330.2 10.0 %collective-permute-start.18 = (bf16[256,256]{1,0:T(8,128)(2,1)S(1)}, bf16[256,256]{1,0:T(8,128)(2,1)S(1)}, u32[]{:S(2)}, u32[]{:S(2)}) collective-permute-start(bf16[256,256]{1,0:T(8,128)(2,1)S(1)} %broadcast_select_fusion.4), channel_id=1, source_target_pairs={{30,0},{31,1},{0,2},{1,3},{2,4},{3,5},{4,6},{5,7},{6,8},{7,9},{8,1... | collective-permute-start | bytes 393224 | tf_op jit(solution)/shard_map/ppermute | solution.py:12
  340.3 7.7 %collective-permute-start.19 = (bf16[256,256]{1,0:T(8,128)(2,1)S(1)}, bf16[256,256]{1,0:T(8,128)(2,1)S(1)}, u32[]{:S(2)}, u32[]{:S(2)}) collective-permute-start(bf16[256,256]{1,0:T(8,128)(2,1)S(1)} %broadcast_select_fusion.7), channel_id=1, source_target_pairs={{28,0},{29,1},{30,2},{31,3},{0,4},{1,5},{2,6},{3,7},{4,8},{5,9},{6... | collective-permute-start | bytes 393224 | tf_op jit(solution)/shard_map/ppermute | solution.py:12
  348.0 6.8 %collective-permute-start.20 = (bf16[256,256]{1,0:T(8,128)(2,1)S(1)}, bf16[256,256]{1,0:T(8,128)(2,1)S(1)}, u32[]{:S(2)}, u32[]{:S(2)}) collective-permute-start(bf16[256,256]{1,0:T(8,128)(2,1)S(1)} %broadcast_select_fusion.10), channel_id=1, source_target_pairs={{24,0},{25,1},{26,2},{27,3},{28,4},{29,5},{30,6},{31,7},{0,8},{1,9... | collective-permute-start | bytes 393224 | tf_op jit(solution)/shard_map/ppermute | solution.py:12
Sparse Core Ops, SparseCore 0:
  13.8 131.7 all-reduce.1
where the time goes:
time: 363 us
  waiting for transfers between devices  301 us (83%)
  starting transfers between devices  18.4 us (5%)
  other arithmetic  18.1 us (5%)
  between operations  15 us (4%)
  matrix products  9.2 us (3%)
    ppermute x21, waiting for transfers between devices, shifted(): return lax.ppermute(block, axis, route)  166 us
    psum x1, waiting for transfers between devices, shards(): lax.psum(jnp.dot(picker, samples, preferred_element_type=jnp.float32), 'b...  135 us
    ppermute x21, starting transfers between devices, shifted(): return lax.ppermute(block, axis, route)  18.3 us
  transfers between devices with their start and end apart: 22, of which 18 were waited for; matrix products, arithmetic and copies ran while one was open for 2% of the time, Pallas kernels for 0%

commit v1 on v0

v1 whole, which is shorter than its diff:
```python
import functools
import math

import jax
import jax.numpy as jnp
from jax import lax
from jax.experimental import pallas as pl
from jax.experimental.pallas import tpu as pltpu
from jax.sharding import PartitionSpec as P

WINDOW = 3
RADIX = 16


def route(block, pairs):
    return lax.ppermute(block, "blk", pairs)


def shifted(block, distance):
    count = lax.axis_size("blk")
    if distance % count == 0:
        return block
    return route(block, [((i - distance) % count, i) for i in range(count)])


def crossed(block, mask):
    return route(block, [(i ^ mask, i) for i in range(lax.axis_size("blk"))])


def plan(offset):
    rest = offset % 4
    far = offset - rest if rest < 2 else offset - rest + 4
    return far, offset - far


def to_stat(rounded, factor):
    values = lax.optimization_barrier(rounded).astype(jnp.float32)
    return factor * (0.5 * (jnp.log1p(values) - jnp.log1p(-values)))


def gather_hubs(parts):
    own = parts[0]
    for k in (1, 2, 3):
        own = own + crossed(parts[k], k)
    mask = 4
    while mask < lax.axis_size("blk"):
        own = own + crossed(own, mask)
        mask *= 2
    return jnp.concatenate([own] + [crossed(own, k) for k in (1, 2, 3)])


def inverse_gram(hub_rows):
    gram = lax.dot_general(
        hub_rows, hub_rows, (((1,), (1,)), ((), ())), preferred_element_type=jnp.float32
    )
    lower = jnp.linalg.cholesky(gram)
    inv_lower = jax.scipy.linalg.solve_triangular(
        lower, jnp.eye(gram.shape[0], dtype=jnp.float32), lower=True
    )
    return jnp.dot(inv_lower.T, inv_lower, precision=lax.Precision.HIGHEST)


def near_blocks(samples, first):
    count = lax.axis_size("blk")
    odd = lax.axis_index("blk") % 2 == 1
    if first == -1:
        return shifted(samples, -1), samples, shifted(samples, 1)
    if first == -2:
        two = shifted(samples, -2)
        one = crossed(jnp.where(odd, samples, two), 1)
        return two, one, samples
    two = shifted(samples, 2)
    one = crossed(jnp.where(odd, two, samples), 1)
    if first == 0:
        return samples, one, two
    three_even = route(samples, [((i - 3) % count, i) for i in range(0, count, 2)])
    three_odd = route(two, [(i, i + 1) for i in range(0, count, 2)])
    return one, two, jnp.where(odd, three_odd, three_even)


def exchange(offset, samples, parts):
    far_distance, first = plan(offset)
    hub_rows = gather_hubs(parts)
    far = shifted(samples, -far_distance)
    near = near_blocks(samples, first)
    return (hub_rows, inverse_gram(hub_rows), far) + near


def give_back(offset, tiles, turned):
    far_distance, first = plan(offset)
    ahead = [shifted(tiles[j], -(first + j)) for j in range(WINDOW)]
    return tuple(ahead), shifted(turned, far_distance)


def residual(x_ref, hub_rows, inverse, out_ref, step):
    proj = lax.dot_general(
        x_ref[...], hub_rows, (((1,), (1,)), ((), ())), preferred_element_type=jnp.float32
    )
    coef = jnp.dot(
        proj, inverse, precision=lax.Precision.HIGHEST, preferred_element_type=jnp.float32
    )
    high = coef.astype(jnp.bfloat16)
    rest = coef - high.astype(jnp.float32)
    mid = rest.astype(jnp.bfloat16)
    low = (rest - mid.astype(jnp.float32)).astype(jnp.bfloat16)
    total = jnp.zeros((x_ref.shape[0], 1), jnp.float32)
    for at in range(0, x_ref.shape[1], step):
        part = hub_rows[:, at:at + step]
        fit = jnp.dot(low, part, preferred_element_type=jnp.float32)
        fit = fit + jnp.dot(mid, part, preferred_element_type=jnp.float32)
        fit = fit + jnp.dot(high, part, preferred_element_type=jnp.float32)
        resid = (x_ref[:, at:at + step].astype(jnp.float32) - fit).astype(jnp.bfloat16)
        out_ref[:, at:at + step] = resid
        wide = resid.astype(jnp.float32)
        total = total + jnp.sum(wide * wide, axis=1, keepdims=True)
    return 1.0 / jnp.sqrt(jnp.maximum(total, 1.0))


def tiles_kernel(
    own_ref, far_ref, near0_ref, near1_ref, near2_ref, hub_ref, inv_ref,
    self_ref, tile_ref, turned_ref, one_ref, two_ref,
):
    hub_rows = hub_ref[...]
    inverse = inv_ref[...]
    step = 512
    rows = own_ref.shape[0]

    def row_of(scale):
        return jnp.transpose(jnp.broadcast_to(scale, (rows, 128)))[0:1, :]

    def corr(left, left_scale, right, right_row):
        dots = lax.dot_general(
            left[...], right[...], (((1,), (1,)), ((), ())), preferred_element_type=jnp.float32
        )
        return dots * left_scale * right_row

    scale = residual(own_ref, hub_rows, inverse, one_ref, step)
    self_ref[...] = corr(one_ref, scale, one_ref, row_of(scale)).astype(jnp.bfloat16)
    far_scale = residual(far_ref, hub_rows, inverse, two_ref, step)
    far_row = row_of(far_scale)
    for j, near_ref in enumerate((near0_ref, near1_ref, near2_ref)):
        scale = residual(near_ref, hub_rows, inverse, one_ref, step)
        tile = corr(one_ref, scale, two_ref, far_row)
        tile_ref[j] = tile.astype(jnp.bfloat16)
        turned_ref[j] = jnp.transpose(tile).astype(jnp.bfloat16)


def make_tiles(own, far, near, hub_rows, inverse):
    rows, width = own.shape
    vmem = pl.BlockSpec(memory_space=pltpu.VMEM)
    return pl.pallas_call(
        tiles_kernel,
        out_shape=(
            jax.ShapeDtypeStruct((rows, rows), jnp.bfloat16),
            jax.ShapeDtypeStruct((WINDOW, rows, rows), jnp.bfloat16),
            jax.ShapeDtypeStruct((WINDOW, rows, rows), jnp.bfloat16),
        ),
        in_specs=[vmem] * 7,
        out_specs=(vmem, vmem, vmem),
        scratch_shapes=[
            pltpu.VMEM((rows, width), jnp.bfloat16),
            pltpu.VMEM((rows, width), jnp.bfloat16),
        ],
        name="tiles",
    )(own, far, *near, hub_rows, inverse)


def shards(samples, hubs, start):
    rows, width = samples.shape
    factor = math.sqrt(width - hubs.shape[0] - 3)
    count = lax.axis_size("blk")
    mine = lax.axis_index("blk")
    offset = start[0]

    quad = jnp.bitwise_xor(mine % 4, jnp.arange(4, dtype=jnp.int32))
    wanted = hubs.reshape(4, -1)[quad].reshape(-1) - mine * rows
    picker = (wanted[:, None] == jnp.arange(rows, dtype=jnp.int32)[None, :]).astype(jnp.bfloat16)
    held = jnp.dot(picker, samples, preferred_element_type=jnp.float32).astype(jnp.bfloat16)
    parts = tuple(jnp.split(held, 4))

    largest = count // 2 - WINDOW
    if largest < RADIX:
        lows, index, highs = range(1, largest + 1), offset - 1, 1
    else:
        lows, index, highs = range(RADIX), offset % RADIX, largest // RADIX + 1
    hops = [functools.partial(shifted, distance=-RADIX * k) for k in range(highs)]
    back_hops = [functools.partial(shifted, distance=RADIX * k) for k in range(highs)]

    hub_rows, inverse, far, *near = lax.switch(
        index, [functools.partial(exchange, low) for low in lows], samples, parts
    )
    if highs > 1:
        far = lax.switch(offset // RADIX, hops, far)

    own, tiles, turned = make_tiles(samples, far, near, hub_rows, inverse)

    ahead, behind = lax.switch(
        index, [functools.partial(give_back, low) for low in lows], tiles, turned
    )
    if highs > 1:
        behind = lax.switch(offset // RADIX, back_hops, behind)

    diag = jnp.arange(rows)[:, None] == jnp.arange(rows)[None, :]
    own_stat = jnp.where(diag, 0.0, to_stat(own, factor))
    ahead = jnp.stack([to_stat(tile, factor) for tile in ahead])
    return (own_stat, ahead, to_stat(behind, factor))


def solution(mesh):
    in_specs = (P("blk", None), P(), P())
    out_specs = (P("blk", None), P(None, "blk", None), P(None, "blk", None))
    return jax.shard_map(shards, mesh=mesh, in_specs=in_specs, out_specs=out_specs, check_vma=False)
```

time: 363 us -> 151 us (0.42)
  the two profiles are of different devices: /device:TPU:0 before, /device:TPU:7 now
where the time goes in v1:
time: 151 us
  waiting for transfers between devices  76.6 us (51%)
  other arithmetic  19.3 us (13%)
  loops' own time  18.8 us (12%)
  starting transfers between devices  16.5 us (11%)
  Pallas kernels  11.8 us (8%)
  local copies, waits for them, and re-layouts  3.67 us (2%)
  matrix products  2.26 us (1%)
  between operations  1.89 us (1%)
    ppermute x15, waiting for transfers between devices, route(): return lax.ppermute(block, 'blk', pairs)  76.6 us
    another operation x1, loops' own time, shards(): lax.switch(index, [functools.partial(exchange, low) for low in lows], sam...  18.7 us
    ppermute x15, starting transfers between devices, route(): return lax.ppermute(block, 'blk', pairs)  16.5 us
    pallas_call x1, Pallas kernels, make_tiles(): pl.pallas_call(tiles_kernel, out_shape=(jax.ShapeDtypeStruct((rows, rows)...  11.8 us
    another operation x3, other arithmetic, inverse_gram(): lower = jnp.linalg.cholesky(gram)  6.52 us
    another operation x2, other arithmetic, inverse_gram(): jax.scipy.linalg.solve_triangular(lower, jnp.eye(gram.shape[0], dtype=jnp...  5.55 us
    another operation x3, other arithmetic, shards(): ahead = jnp.stack([to_stat(tile, factor) for tile in ahead])  3.37 us
  transfers between devices with their start and end apart: 15, of which 9 were waited for; matrix products, arithmetic and copies ran while one was open for 11% of the time, Pallas kernels for 0%

profile of v1, /device:TPU:7, one launch (start us, length us, event | category | flops | bytes accessed | tf_op | source)
XLA Modules:
  0.0 150.8 jit_solution(18433407911571222327)
XLA Ops:
  2.8 1.6 %convolution_convert_fusion = bf16[64,2048]{1,0:T(8,128)(2,1)S(1)} fusion(bf16[256,2048]{1,0:T(8,128)(2,1)} %own_ref.1, s32[64]{0:T(128)S(1)} %sub.34), kind=kOutput, calls=%fused_computation.223 | convolution fusion | flops 67256320 | bytes 1310976 | tf_op jit(solution)/shard_map/dot_general | solution.py:178
  4.4 110.7 %conditional.2 = (bf16[64,2048]{1,0:T(8,128)(2,1)}, f32[64,64]{1,0:T(8,128)S(1)}, bf16[256,2048]{1,0:T(8,128)(2,1)}, bf16[256,2048]{1,0:T(8,128)(2,1)}, bf16[256...) conditional(s32[]{:T(128)} %bitcast.78, (bf16[16,2048]{1,0:T(8,128)(2,1)S(1)}, ...), branch_computations={%region_0.5_spmd, %region_3.6_spmd, %region_4.7_spmd, %region_5.8_... | conditional | flops 25407552 | bytes 32589064 | solution.py:189
  23.8 1.5 collective-permute-start.181
  25.2 1.2 collective-permute-start.189
  27.1 2.2 %collective-permute-done.181 = bf16[16,2048]{1,0:T(8,128)(2,1)S(1)} collective-permute-done((bf16[16,2048]{1,0:T(8,128)(2,1)S(1)}, bf16[16,2048]{1,0:T(8,128)(2,1)S(1)}, u32[]{:S(2)}, u32[]{:S(2)}) %collective-permute-start.181) | collective-permute-done | bytes 65568 | tf_op jit(solution)/shard_map/cond/branch_11_fun/ppermute | solution.py:16
  29.6 3.9 %collective-permute-done.182 = bf16[16,2048]{1,0:T(8,128)(2,1)S(1)} collective-permute-done((bf16[16,2048]{1,0:T(8,128)(2,1)S(1)}, bf16[16,2048]{1,0:T(8,128)(2,1)S(1)}, u32[]{:S(2)}, u32[]{:S(2)}) %collective-permute-start.182) | collective-permute-done | bytes 65568 | tf_op jit(solution)/shard_map/cond/branch_11_fun/ppermute | solution.py:16
  34.3 19.3 %collective-permute-done.183 = bf16[16,2048]{1,0:T(8,128)(2,1)S(1)} collective-permute-done((bf16[16,2048]{1,0:T(8,128)(2,1)S(1)}, bf16[16,2048]{1,0:T(8,128)(2,1)S(1)}, u32[]{:S(2)}, u32[]{:S(2)}) %collective-permute-start.183) | collective-permute-done | bytes 65568 | tf_op jit(solution)/shard_map/cond/branch_11_fun/ppermute | solution.py:16
  53.8 5.3 %collective-permute-done.184 = bf16[16,2048]{1,0:T(8,128)(2,1)S(1)} collective-permute-done((bf16[16,2048]{1,0:T(8,128)(2,1)S(1)}, bf16[16,2048]{1,0:T(8,128)(2,1)S(1)}, u32[]{:S(2)}, u32[]{:S(2)}) %collective-permute-start.184) | collective-permute-done | bytes 65568 | tf_op jit(solution)/shard_map/cond/branch_11_fun/ppermute | solution.py:16
  59.2 6.3 %collective-permute-start.187 = (bf16[16,2048]{1,0:T(8,128)(2,1)S(1)}, bf16[16,2048]{1,0:T(8,128)(2,1)S(1)}, u32[]{:S(2)}, u32[]{:S(2)}) collective-permute-start(bf16[16,2048]{1,0:T(8,128)(2,1)S(1)} %add.278), channel_id=1, source_target_pairs={{3,0},{2,1},{1,2},{0,3},{7,4},{6,5},{5,6},{4,7},{11,8},{10,9},{9,1... | collective-permute-start | bytes 196616 | tf_op jit(solution)/shard_map/cond/branch_11_fun/ppermute | solution.py:16
  66.0 2.6 %collective-permute-start.188 = (bf16[256,2048]{1,0:T(8,128)(2,1)S(1)}, bf16[256,2048]{1,0:T(8,128)(2,1)}, u32[]{:S(2)}, u32[]{:S(2)}) collective-permute-start(bf16[256,2048]{1,0:T(8,128)(2,1)S(1)} %get-tuple-element.418), channel_id=1, source_target_pairs={{12,0},{13,1},{14,2},{15,3},{16,4},{17,5},{18,6},{19,7},{20,8},{21... | collective-permute-start | bytes 3145736 | tf_op jit(solution)/shard_map/cond/branch_11_fun/ppermute | solution.py:16
  68.6 1.0 copy.88
  70.4 1.3 broadcast_select_fusion.11
  71.9 5.8 %cholesky.330 = f32[64,64]{1,0:T(8,128)S(1)} custom-call(f32[64,64]{1,0:T(8,128)S(1)} %fusion.69), custom_call_target="Cholesky" | custom-call | tf_op jit(solution)/shard_map/cond/branch_11_fun/jit(cholesky)/cholesky | solution.py:56
  79.1 4.9 %custom-call.28 = f32[1,64,64]{1,2,0:T(8,128)S(1)} custom-call(f32[1,64,64]{2,1,0:T(8,128)S(1)} %fusion.66), custom_call_target="InvertDiagBlocksLowerTriangular" | custom-call | tf_op jit(solution)/shard_map/cond/branch_11_fun/jit(_solve_triangular)/triangular_solve | solution.py:57
  84.5 30.4 %collective-permute-done.188 = bf16[256,2048]{1,0:T(8,128)(2,1)} collective-permute-done((bf16[256,2048]{1,0:T(8,128)(2,1)S(1)}, bf16[256,2048]{1,0:T(8,128)(2,1)}, u32[]{:S(2)}, u32[]{:S(2)}) %collective-permute-start.188) | collective-permute-done | bytes 1048608 | tf_op jit(solution)/shard_map/cond/branch_11_fun/ppermute | solution.py:16
  115.1 11.8 %tiles.1 = (bf16[256,256]{1,0:T(8,128)(2,1)}, bf16[3,256,256]{2,1,0:T(8,128)(2,1)S(1)}, bf16[3,256,256]{2,1,0:T(8,128)(2,1)S(1)}) custom-call(bf16[256,2048]{1,0:T(8,128)(2,1)S(1)} %copy-done, bf16[256,2048]{1,0:T(8,128)(2,1)} %get-tuple-element.291.far_ref, bf16[256,2048]{1,0:T(8,128)(2,1)} %get-tuple-element.292.near0_ref, ...), custom_call_target="tpu_custom_call" | custom-call | tf_op jit(solution)/shard_map/tiles/pallas_call | solution.py:151
  126.9 17.7 %conditional.3 = (bf16[256,256]{1,0:T(8,128)(2,1)}, bf16[256,256]{1,0:T(8,128)(2,1)}, bf16[256,256]{1,0:T(8,128)(2,1)}, bf16[3,256,256]{2,1,0:T(8,128)(2,1)S(1)}) conditional(s32[]{:T(128)} %bitcast.78, (bf16[3,256,256]{2,1,0:T(8,128)(2,1)S(1)}, bf16[3,256,256]{2,1,0:T(8,128)(2,1)S(1)}) %tuple.115, ...), branch_computations={%region_15.18_spmd, %region_16.19_spmd, %region_17.20_spmd, %regio... | conditional | bytes 4718784 | solution.py:197
  127.7 1.3 collective-permute-start.36
  129.7 11.1 %collective-permute-done.37 = bf16[3,256,256]{2,1,0:T(8,128)(2,1)S(1)} collective-permute-done((bf16[3,256,256]{2,1,0:T(8,128)(2,1)S(1)}, bf16[3,256,256]{2,1,0:T(8,128)(2,1)S(1)}, u32[]{:S(2)}, u32[]{:S(2)}) %collective-permute-start.37) | collective-permute-done | bytes 393248 | tf_op jit(solution)/shard_map/cond/branch_11_fun/ppermute | solution.py:16
  140.9 1.4 collective-permute-done.36
  142.3 2.3 %collective-permute-done.35 = bf16[256,256]{1,0:T(8,128)(2,1)} collective-permute-done((bf16[256,256]{1,0:T(8,128)(2,1)S(1)}, bf16[256,256]{1,0:T(8,128)(2,1)}, u32[]{:S(2)}, u32[]{:S(2)}) %collective-permute-start.35) | collective-permute-done | bytes 131104 | tf_op jit(solution)/shard_map/cond/branch_11_fun/ppermute | solution.py:16
  145.5 1.1 fusion.95
  146.6 1.3 fusion.87
  148.9 1.4 fusion.79
  (47 shorter events, 10.9 us)
Async XLA Ops:
  0.6 3.8 %copy-start = (bf16[256,2048]{1,0:T(8,128)(2,1)S(1)}, bf16[256,2048]{1,0:T(8,128)(2,1)}, u32[]{:S(2)}) copy-start(bf16[256,2048]{1,0:T(8,128)(2,1)} %own_ref.1) | copy-start | bytes 3145732
  22.8 3.7 %collective-permute-start.179 = (bf16[16,2048]{1,0:T(8,128)(2,1)S(1)}, bf16[16,2048]{1,0:T(8,128)(2,1)S(1)}, u32[]{:S(2)}, u32[]{:S(2)}) collective-permute-start(bf16[16,2048]{1,0:T(8,128)(2,1)S(1)} %get-tuple-element.240), channel_id=1, source_target_pairs={{1,0},{0,1},{3,2},{2,3},{5,4},{4,5},{7,6},{6,7},{9,8},{8,9},{11,10... | collective-permute-start | bytes 196616 | tf_op jit(solution)/shard_map/cond/branch_11_fun/ppermute | solution.py:16
  23.5 3.6 %collective-permute-start.180 = (bf16[16,2048]{1,0:T(8,128)(2,1)S(1)}, bf16[16,2048]{1,0:T(8,128)(2,1)S(1)}, u32[]{:S(2)}, u32[]{:S(2)}) collective-permute-start(bf16[16,2048]{1,0:T(8,128)(2,1)S(1)} %get-tuple-element.241), channel_id=1, source_target_pairs={{2,0},{3,1},{0,2},{1,3},{6,4},{7,5},{4,6},{5,7},{10,8},{11,9},{8,1... | collective-permute-start | bytes 196616 | tf_op jit(solution)/shard_map/cond/branch_11_fun/ppermute | solution.py:16
  23.8 5.5 %collective-permute-start.181 = (bf16[16,2048]{1,0:T(8,128)(2,1)S(1)}, bf16[16,2048]{1,0:T(8,128)(2,1)S(1)}, u32[]{:S(2)}, u32[]{:S(2)}) collective-permute-start(bf16[16,2048]{1,0:T(8,128)(2,1)S(1)} %get-tuple-element.242), channel_id=1, source_target_pairs={{3,0},{2,1},{1,2},{0,3},{7,4},{6,5},{5,6},{4,7},{11,8},{10,9},{9,1... | collective-permute-start | bytes 196616 | tf_op jit(solution)/shard_map/cond/branch_11_fun/ppermute | solution.py:16
  25.2 45.2 %collective-permute-start.189 = (bf16[256,2048]{1,0:T(8,128)(2,1)S(1)}, bf16[256,2048]{1,0:T(8,128)(2,1)}, u32[]{:S(2)}, u32[]{:S(2)}) collective-permute-start(bf16[256,2048]{1,0:T(8,128)(2,1)S(1)} %get-tuple-element.418), channel_id=1, source_target_pairs={{30,0},{31,1},{0,2},{1,3},{2,4},{3,5},{4,6},{5,7},{6,8},{7,9},{8,1... | collective-permute-start | bytes 3145736 | tf_op jit(solution)/shard_map/cond/branch_11_fun/ppermute | solution.py:16
  29.3 4.2 %collective-permute-start.182 = (bf16[16,2048]{1,0:T(8,128)(2,1)S(1)}, bf16[16,2048]{1,0:T(8,128)(2,1)S(1)}, u32[]{:S(2)}, u32[]{:S(2)}) collective-permute-start(bf16[16,2048]{1,0:T(8,128)(2,1)S(1)} %add_add_fusion.11), channel_id=1, source_target_pairs={{4,0},{5,1},{6,2},{7,3},{0,4},{1,5},{2,6},{3,7},{12,8},{13,9},{14,... | collective-permute-start | bytes 196616 | tf_op jit(solution)/shard_map/cond/branch_11_fun/ppermute | solution.py:16
  33.6 20.0 %collective-permute-start.183 = (bf16[16,2048]{1,0:T(8,128)(2,1)S(1)}, bf16[16,2048]{1,0:T(8,128)(2,1)S(1)}, u32[]{:S(2)}, u32[]{:S(2)}) collective-permute-start(bf16[16,2048]{1,0:T(8,128)(2,1)S(1)} %add.276), channel_id=1, source_target_pairs={{8,0},{9,1},{10,2},{11,3},{12,4},{13,5},{14,6},{15,7},{0,8},{1,9},... | collective-permute-start | bytes 196616 | tf_op jit(solution)/shard_map/cond/branch_11_fun/ppermute | solution.py:16
  53.6 5.5 %collective-permute-start.184 = (bf16[16,2048]{1,0:T(8,128)(2,1)S(1)}, bf16[16,2048]{1,0:T(8,128)(2,1)S(1)}, u32[]{:S(2)}, u32[]{:S(2)}) collective-permute-start(bf16[16,2048]{1,0:T(8,128)(2,1)S(1)} %add.277), channel_id=1, source_target_pairs={{16,0},{17,1},{18,2},{19,3},{20,4},{21,5},{22,6},{23,7},{24,8},{25... | collective-permute-start | bytes 196616 | tf_op jit(solution)/shard_map/cond/branch_11_fun/ppermute | solution.py:16
  59.2 10.5 %collective-permute-start.187 = (bf16[16,2048]{1,0:T(8,128)(2,1)S(1)}, bf16[16,2048]{1,0:T(8,128)(2,1)S(1)}, u32[]{:S(2)}, u32[]{:S(2)}) collective-permute-start(bf16[16,2048]{1,0:T(8,128)(2,1)S(1)} %add.278), channel_id=1, source_target_pairs={{3,0},{2,1},{1,2},{0,3},{7,4},{6,5},{5,6},{4,7},{11,8},{10,9},{9,1... | collective-permute-start | bytes 196616 | tf_op jit(solution)/shard_map/cond/branch_11_fun/ppermute | solution.py:16
  65.5 4.1 %collective-permute-start.186 = (bf16[16,2048]{1,0:T(8,128)(2,1)S(1)}, bf16[16,2048]{1,0:T(8,128)(2,1)S(1)}, u32[]{:S(2)}, u32[]{:S(2)}) collective-permute-start(bf16[16,2048]{1,0:T(8,128)(2,1)S(1)} %add.278), channel_id=1, source_target_pairs={{2,0},{3,1},{0,2},{1,3},{6,4},{7,5},{4,6},{5,7},{10,8},{11,9},{8,1... | collective-permute-start | bytes 196616 | tf_op jit(solution)/shard_map/cond/branch_11_fun/ppermute | solution.py:16
  65.5 4.1 %collective-permute-start.185 = (bf16[16,2048]{1,0:T(8,128)(2,1)S(1)}, bf16[16,2048]{1,0:T(8,128)(2,1)S(1)}, u32[]{:S(2)}, u32[]{:S(2)}) collective-permute-start(bf16[16,2048]{1,0:T(8,128)(2,1)S(1)} %add.278), channel_id=1, source_target_pairs={{1,0},{0,1},{3,2},{2,3},{5,4},{4,5},{7,6},{6,7},{9,8},{8,9},{11,10... | collective-permute-start | bytes 196616 | tf_op jit(solution)/shard_map/cond/branch_11_fun/ppermute | solution.py:16
  66.0 48.9 %collective-permute-start.188 = (bf16[256,2048]{1,0:T(8,128)(2,1)S(1)}, bf16[256,2048]{1,0:T(8,128)(2,1)}, u32[]{:S(2)}, u32[]{:S(2)}) collective-permute-start(bf16[256,2048]{1,0:T(8,128)(2,1)S(1)} %get-tuple-element.418), channel_id=1, source_target_pairs={{12,0},{13,1},{14,2},{15,3},{16,4},{17,5},{18,6},{19,7},{20,8},{21... | collective-permute-start | bytes 3145736 | tf_op jit(solution)/shard_map/cond/branch_11_fun/ppermute | solution.py:16
  69.7 0.7 copy-start.12
  71.8 43.1 %collective-permute-start.190 = (bf16[256,2048]{1,0:T(8,128)(2,1)S(1)}, bf16[256,2048]{1,0:T(8,128)(2,1)}, u32[]{:S(2)}, u32[]{:S(2)}) collective-permute-start(bf16[256,2048]{1,0:T(8,128)(2,1)S(1)} %broadcast_select_fusion.11), channel_id=1, source_target_pairs={{1,0},{0,1},{3,2},{2,3},{5,4},{4,5},{7,6},{6,7},{9,8},{8,9},{11,10... | collective-permute-start | bytes 3145736 | tf_op jit(solution)/shard_map/cond/branch_11_fun/ppermute | solution.py:16
  126.9 17.8 %copy-start.14 = (bf16[256,256]{1,0:T(8,128)(2,1)S(1)}, bf16[256,256]{1,0:T(8,128)(2,1)}, u32[]{:S(2)}) copy-start(bf16[256,256]{1,0:T(8,128)(2,1)} %get-tuple-element.297) | copy-start | bytes 393220
  126.9 13.9 %collective-permute-start.37 = (bf16[3,256,256]{2,1,0:T(8,128)(2,1)S(1)}, bf16[3,256,256]{2,1,0:T(8,128)(2,1)S(1)}, u32[]{:S(2)}, u32[]{:S(2)}) collective-permute-start(bf16[3,256,256]{2,1,0:T(8,128)(2,1)S(1)} %get-tuple-element.272), channel_id=1, source_target_pairs={{20,0},{21,1},{22,2},{23,3},{24,4},{25,5},{26,6},{27,7},{28,8},{29... | collective-permute-start | bytes 1179656 | tf_op jit(solution)/shard_map/cond/branch_11_fun/ppermute | solution.py:16
  127.7 14.6 %collective-permute-start.36 = (bf16[256,256]{1,0:T(8,128)(2,1)S(1)}, bf16[256,256]{1,0:T(8,128)(2,1)}, u32[]{:S(2)}, u32[]{:S(2)}) collective-permute-start(bf16[256,256]{1,0:T(8,128)(2,1)S(1)} %get-tuple-element.337), channel_id=1, source_target_pairs={{2,0},{3,1},{4,2},{5,3},{6,4},{7,5},{8,6},{9,7},{10,8},{11,9},{12,... | collective-permute-start | bytes 393224 | tf_op jit(solution)/shard_map/cond/branch_11_fun/ppermute | solution.py:16
  129.0 15.7 %collective-permute-start.35 = (bf16[256,256]{1,0:T(8,128)(2,1)S(1)}, bf16[256,256]{1,0:T(8,128)(2,1)}, u32[]{:S(2)}, u32[]{:S(2)}) collective-permute-start(bf16[256,256]{1,0:T(8,128)(2,1)S(1)} %get-tuple-element.338), channel_id=1, source_target_pairs={{1,0},{2,1},{3,2},{4,3},{5,4},{6,5},{7,6},{8,7},{9,8},{10,9},{11,1... | collective-permute-start | bytes 393224 | tf_op jit(solution)/shard_map/cond/branch_11_fun/ppermute | solution.py:16

commit v2 on v1

v2 whole, which is shorter than its diff:
```python
import functools
import math

import jax
import jax.numpy as jnp
from jax import lax
from jax.experimental import pallas as pl
from jax.experimental.pallas import tpu as pltpu
from jax.sharding import PartitionSpec as P

WINDOW = 3
RADIX = 16


def route(block, pairs):
    return lax.ppermute(block, "blk", pairs)


def shifted(block, distance):
    count = lax.axis_size("blk")
    if distance % count == 0:
        return block
    return route(block, [((i - distance) % count, i) for i in range(count)])


def crossed(block, mask):
    return route(block, [(i ^ mask, i) for i in range(lax.axis_size("blk"))])


def to_stat(rounded, factor):
    values = rounded.astype(jnp.float32)
    return factor * (0.5 * (jnp.log1p(values) - jnp.log1p(-values)))


def gather_hubs(parts):
    own = parts[0]
    for k in (1, 2, 3):
        own = own + crossed(parts[k], k)
    mask = 4
    while mask < lax.axis_size("blk"):
        own = own + crossed(own, mask)
        mask *= 2
    return jnp.concatenate([own] + [crossed(own, k) for k in (1, 2, 3)])


def inverse_gram(hub_rows):
    gram = lax.dot_general(
        hub_rows, hub_rows, (((1,), (1,)), ((), ())), preferred_element_type=jnp.float32
    )
    across = lax.broadcasted_iota(jnp.int32, gram.shape, 1)
    down = lax.broadcasted_iota(jnp.int32, gram.shape, 0)

    def sweep(k, held):
        in_row, in_col = down == k, across == k
        row = jnp.sum(jnp.where(in_row, held, 0.0), axis=0, keepdims=True)
        col = jnp.sum(jnp.where(in_col, held, 0.0), axis=1, keepdims=True)
        pivot = 1.0 / jnp.sum(jnp.where(across[0:1] == k, row, 0.0), axis=1, keepdims=True)
        scaled = row * pivot
        new = jnp.where(in_col, col * pivot, held - col * scaled)
        new = jnp.where(in_row, scaled, new)
        return jnp.where(jnp.logical_and(in_row, in_col), -pivot, new)

    return -lax.fori_loop(0, gram.shape[0], sweep, gram)


def pieces(proj, inverse):
    coef = jnp.dot(
        proj, inverse, precision=lax.Precision.HIGHEST, preferred_element_type=jnp.float32
    )
    high = coef.astype(jnp.bfloat16)
    rest = coef - high.astype(jnp.float32)
    mid = rest.astype(jnp.bfloat16)
    low = (rest - mid.astype(jnp.float32)).astype(jnp.bfloat16)
    return jnp.concatenate([high, mid, low], axis=1)


def loop(steps, body, init, rolled):
    if rolled:
        return lax.fori_loop(0, steps, body, init)
    for k in range(steps):
        init = body(k, init)
    return init


def residual(x_ref, hub_ref, inverse, out_ref, step, rolled):
    rows, width = x_ref.shape

    def at(k):
        return pl.ds(pl.multiple_of(k * step, step) if rolled else k * step, step)

    def project(k, proj):
        return proj + lax.dot_general(
            x_ref[:, at(k)], hub_ref[:, at(k)], (((1,), (1,)), ((), ())),
            preferred_element_type=jnp.float32,
        )

    if rolled:
        proj = loop(
            width // step, project, jnp.zeros((rows, hub_ref.shape[0]), jnp.float32), rolled
        )
    else:
        proj = lax.dot_general(
            x_ref[...], hub_ref[...], (((1,), (1,)), ((), ())), preferred_element_type=jnp.float32
        )
    coef = pieces(proj, inverse)

    def subtract(k, total):
        part = hub_ref[:, at(k)]
        fit = jnp.dot(
            coef, jnp.concatenate([part] * 3, axis=0), preferred_element_type=jnp.float32
        )
        resid = (x_ref[:, at(k)].astype(jnp.float32) - fit).astype(jnp.bfloat16)
        out_ref[:, at(k)] = resid
        wide = resid.astype(jnp.float32)
        square = wide * wide
        for lane in range(0, step, 128):
            total = total + square[:, lane:lane + 128]
        return total

    total = loop(width // step, subtract, jnp.zeros((rows, 128), jnp.float32), rolled)
    total = jnp.sum(total, axis=1, keepdims=True)
    return 1.0 / jnp.sqrt(jnp.maximum(total, 1.0))


def as_row(scale):
    return jnp.transpose(jnp.broadcast_to(scale, (scale.shape[0], 128)))[0:1, :]


def correlation(left_ref, left_scale, right_ref, right_row, step, rolled):
    rows, width = left_ref.shape

    def add(k, dots):
        at = pl.ds(pl.multiple_of(k * step, step) if rolled else k * step, step)
        return dots + lax.dot_general(
            left_ref[:, at], right_ref[:, at], (((1,), (1,)), ((), ())),
            preferred_element_type=jnp.float32,
        )

    if rolled:
        dots = loop(width // step, add, jnp.zeros((rows, rows), jnp.float32), rolled)
    else:
        dots = lax.dot_general(
            left_ref[...], right_ref[...], (((1,), (1,)), ((), ())),
            preferred_element_type=jnp.float32,
        )
    return dots * left_scale * right_row


def own_kernel(factor, own_ref, hub_ref, inv_ref, self_ref, resid_ref, scale_ref):
    inverse = inverse_gram(hub_ref[...])
    inv_ref[...] = inverse
    scale = residual(own_ref, hub_ref, inverse, resid_ref, 256, True)
    scale_ref[...] = scale
    tile = correlation(resid_ref, scale, resid_ref, as_row(scale), 256, True)
    stat = to_stat(tile.astype(jnp.bfloat16), factor)
    down = lax.broadcasted_iota(jnp.int32, stat.shape, 0)
    across = lax.broadcasted_iota(jnp.int32, stat.shape, 1)
    self_ref[...] = jnp.where(down == across, 0.0, stat)


def own_tile(own, hub_rows, factor):
    rows, width = own.shape
    hubs = hub_rows.shape[0]
    vmem = pl.BlockSpec(memory_space=pltpu.VMEM)
    return pl.pallas_call(
        functools.partial(own_kernel, factor),
        out_shape=(
            jax.ShapeDtypeStruct((hubs, hubs), jnp.float32),
            jax.ShapeDtypeStruct((rows, rows), jnp.float32),
            jax.ShapeDtypeStruct((rows, width), jnp.bfloat16),
            jax.ShapeDtypeStruct((rows, 1), jnp.float32),
        ),
        in_specs=[vmem] * 2,
        out_specs=(vmem,) * 4,
        cost_estimate=pl.CostEstimate(
            flops=20 * 10**9, bytes_accessed=2 * rows * width, transcendentals=0
        ),
        name="own_tile",
    )(own, hub_rows)


def tiles_kernel(
    far_ref, next_ref, own_ref, scale_ref, last_ref, hub_ref, inv_ref,
    tile_ref, turned_ref, one_ref, two_ref,
):
    inverse = inv_ref[...]
    far_row = as_row(residual(far_ref, hub_ref, inverse, two_ref, 512, False))
    for j, near_ref in enumerate((next_ref, None, last_ref)):
        if near_ref is None:
            left, scale = own_ref, scale_ref[...]
        else:
            left, scale = one_ref, residual(near_ref, hub_ref, inverse, one_ref, 512, False)
        tile = correlation(left, scale, two_ref, far_row, 512, False)
        tile_ref[j] = tile.astype(jnp.bfloat16)
        turned_ref[j] = jnp.transpose(tile).astype(jnp.bfloat16)


def make_tiles(far, *rest):
    rows, width = far.shape
    vmem = pl.BlockSpec(memory_space=pltpu.VMEM)
    return pl.pallas_call(
        tiles_kernel,
        out_shape=(jax.ShapeDtypeStruct((WINDOW, rows, rows), jnp.bfloat16),) * 2,
        in_specs=[vmem] * 7,
        out_specs=(vmem,) * 2,
        scratch_shapes=[pltpu.VMEM((rows, width), jnp.bfloat16)] * 2,
        name="tiles",
    )(far, *rest)


def stats_kernel(factor, next_ref, own_ref, last_ref, back_ref, ahead_ref, behind_ref):
    for j, tile_ref in enumerate((next_ref, own_ref, last_ref)):
        ahead_ref[j] = to_stat(tile_ref[...], factor)
        behind_ref[j] = to_stat(back_ref[j], factor)


def make_stats(ahead, back, factor):
    vmem = pl.BlockSpec(memory_space=pltpu.VMEM)
    return pl.pallas_call(
        functools.partial(stats_kernel, factor),
        out_shape=(jax.ShapeDtypeStruct(back.shape, jnp.float32),) * 2,
        in_specs=[vmem] * 4,
        out_specs=(vmem,) * 2,
        name="stats",
    )(*ahead, back)


def exchange(offset, samples, hub_rows, factor):
    far = shifted(samples, -(offset + 1))
    following = shifted(samples, -1)
    previous = shifted(samples, 1)
    return own_tile(samples, hub_rows, factor) + (far, following, previous)


def give_back(offset, tiles, turned):
    ahead = (shifted(tiles[0], 1), tiles[1], shifted(tiles[2], -1))
    return ahead, shifted(turned, offset + 1)


def shards(samples, hubs, start):
    rows, width = samples.shape
    factor = math.sqrt(width - hubs.shape[0] - 3)
    count = lax.axis_size("blk")
    mine = lax.axis_index("blk")
    offset = start[0]

    quad = jnp.bitwise_xor(mine % 4, jnp.arange(4, dtype=jnp.int32))
    wanted = hubs.reshape(4, -1)[quad].reshape(-1) - mine * rows
    picker = (wanted[:, None] == jnp.arange(rows, dtype=jnp.int32)[None, :]).astype(jnp.bfloat16)
    held = jnp.dot(picker, samples, preferred_element_type=jnp.float32).astype(jnp.bfloat16)
    parts = tuple(jnp.split(held, 4))

    largest = count // 2 - WINDOW
    if largest < RADIX:
        lows, index, highs = range(1, largest + 1), offset - 1, 1
    else:
        lows, index, highs = range(RADIX), offset % RADIX, largest // RADIX + 1
    hops = [functools.partial(shifted, distance=-RADIX * k) for k in range(highs)]
    back_hops = [functools.partial(shifted, distance=RADIX * k) for k in range(highs)]

    hub_rows = gather_hubs(parts)
    inverse, own_stat, own, scale, far, following, previous = lax.switch(
        index, [functools.partial(exchange, low, factor=factor) for low in lows],
        samples, hub_rows,
    )
    if highs > 1:
        far = lax.switch(offset // RADIX, hops, far)

    tiles, turned = make_tiles(far, following, own, scale, previous, hub_rows, inverse)

    ahead, back = lax.switch(
        index, [functools.partial(give_back, low) for low in lows], tiles, turned
    )
    if highs > 1:
        back = lax.switch(offset // RADIX, back_hops, back)
    return (own_stat,) + tuple(make_stats(ahead, back, factor))


def solution(mesh):
    in_specs = (P("blk", None), P(), P())
    out_specs = (P("blk", None), P(None, "blk", None), P(None, "blk", None))
    return jax.shard_map(shards, mesh=mesh, in_specs=in_specs, out_specs=out_specs, check_vma=False)
```

time: 151 us -> 96 us (0.64)
  the two profiles are of different devices: /device:TPU:7 before, /device:TPU:0 now
where the time goes in v2:
time: 96 us; the launch traced here: 94.7 us
  waiting for transfers between devices  47 us (49%)
  Pallas kernels  23.8 us (25%)
  starting transfers between devices  18.7 us (19%)
  local copies, waits for them, and re-layouts  2.06 us (2%)
  matrix products  1.56 us (2%)
  between operations  1.4 us (1%)
    ppermute x15, waiting for transfers between devices, route(): return lax.ppermute(block, 'blk', pairs)  47 us
    ppermute x15, starting transfers between devices, route(): return lax.ppermute(block, 'blk', pairs)  18.7 us
    pallas_call x1, Pallas kernels, own_tile(): pl.pallas_call(functools.partial(own_kernel, factor), out_shape=(jax.Shap...  13.6 us
    pallas_call x1, Pallas kernels, make_tiles(): pl.pallas_call(tiles_kernel, out_shape=(jax.ShapeDtypeStruct((WINDOW, row...  6.93 us
    pallas_call x1, Pallas kernels, make_stats(): pl.pallas_call(functools.partial(stats_kernel, factor), out_shape=(jax.Sh...  3.31 us
  transfers between devices with their start and end apart: 15, of which 12 were waited for; matrix products, arithmetic and copies ran while one was open for 0% of the time, Pallas kernels for 14%

profile of v2, /device:TPU:0, one launch (start us, length us, event | category | flops | bytes accessed | tf_op | source)
XLA Modules:
  0.0 94.7 jit_solution(10999511622093278614)
XLA Ops:
  2.0 1.6 %convolution_convert_fusion = bf16[64,2048]{1,0:T(8,128)(2,1)S(1)} fusion(bf16[256,2048]{1,0:T(8,128)(2,1)} %param.29, s32[64]{0:T(128)S(1)} %sub.19), kind=kOutput, calls=%fused_computation.27 | convolution fusion | flops 67256320 | bytes 1310976 | tf_op jit(solution)/shard_map/dot_general | solution.py:250
  4.2 2.6 %collective-permute-start.80 = (bf16[16,2048]{1,0:T(8,128)(2,1)S(1)}, bf16[16,2048]{1,0:T(8,128)(2,1)S(1)}, u32[]{:S(2)}, u32[]{:S(2)}) collective-permute-start(bf16[16,2048]{1,0:T(8,128)(2,1)S(1)} %get-tuple-element.269), channel_id=1, source_target_pairs={{3,0},{2,1},{1,2},{0,3},{7,4},{6,5},{5,6},{4,7},{11,8},{10,9},{9,1... | collective-permute-start | bytes 196616 | tf_op jit(solution)/shard_map/ppermute | solution.py:16
  6.8 2.4 %collective-permute-done.80 = bf16[16,2048]{1,0:T(8,128)(2,1)S(1)} collective-permute-done((bf16[16,2048]{1,0:T(8,128)(2,1)S(1)}, bf16[16,2048]{1,0:T(8,128)(2,1)S(1)}, u32[]{:S(2)}, u32[]{:S(2)}) %collective-permute-start.80) | collective-permute-done | bytes 65568 | tf_op jit(solution)/shard_map/ppermute | solution.py:16
  9.3 1.8 %collective-permute-done.79 = bf16[16,2048]{1,0:T(8,128)(2,1)S(1)} collective-permute-done((bf16[16,2048]{1,0:T(8,128)(2,1)S(1)}, bf16[16,2048]{1,0:T(8,128)(2,1)S(1)}, u32[]{:S(2)}, u32[]{:S(2)}) %collective-permute-start.79) | collective-permute-done | bytes 65568 | tf_op jit(solution)/shard_map/ppermute | solution.py:16
  11.1 1.6 %collective-permute-start.81 = (bf16[16,2048]{1,0:T(8,128)(2,1)S(1)}, bf16[16,2048]{1,0:T(8,128)(2,1)S(1)}, u32[]{:S(2)}, u32[]{:S(2)}) collective-permute-start(bf16[16,2048]{1,0:T(8,128)(2,1)S(1)} %fusion.1), channel_id=1, source_target_pairs={{4,0},{5,1},{6,2},{7,3},{0,4},{1,5},{2,6},{3,7},{12,8},{13,9},{14,... | collective-permute-start | bytes 196616 | tf_op jit(solution)/shard_map/ppermute | solution.py:16
  12.7 2.7 %collective-permute-done.81 = bf16[16,2048]{1,0:T(8,128)(2,1)S(1)} collective-permute-done((bf16[16,2048]{1,0:T(8,128)(2,1)S(1)}, bf16[16,2048]{1,0:T(8,128)(2,1)S(1)}, u32[]{:S(2)}, u32[]{:S(2)}) %collective-permute-start.81) | collective-permute-done | bytes 65568 | tf_op jit(solution)/shard_map/ppermute | solution.py:16
  15.4 1.6 %collective-permute-start.82 = (bf16[16,2048]{1,0:T(8,128)(2,1)S(1)}, bf16[16,2048]{1,0:T(8,128)(2,1)S(1)}, u32[]{:S(2)}, u32[]{:S(2)}) collective-permute-start(bf16[16,2048]{1,0:T(8,128)(2,1)S(1)} %add.39), channel_id=1, source_target_pairs={{8,0},{9,1},{10,2},{11,3},{12,4},{13,5},{14,6},{15,7},{0,8},{1,9},... | collective-permute-start | bytes 196616 | tf_op jit(solution)/shard_map/ppermute | solution.py:16
  17.1 2.7 %collective-permute-done.82 = bf16[16,2048]{1,0:T(8,128)(2,1)S(1)} collective-permute-done((bf16[16,2048]{1,0:T(8,128)(2,1)S(1)}, bf16[16,2048]{1,0:T(8,128)(2,1)S(1)}, u32[]{:S(2)}, u32[]{:S(2)}) %collective-permute-start.82) | collective-permute-done | bytes 65568 | tf_op jit(solution)/shard_map/ppermute | solution.py:16
  19.8 3.3 %collective-permute-start.83 = (bf16[16,2048]{1,0:T(8,128)(2,1)S(1)}, bf16[16,2048]{1,0:T(8,128)(2,1)S(1)}, u32[]{:S(2)}, u32[]{:S(2)}) collective-permute-start(bf16[16,2048]{1,0:T(8,128)(2,1)S(1)} %add.40), channel_id=1, source_target_pairs={{16,0},{17,1},{18,2},{19,3},{20,4},{21,5},{22,6},{23,7},{24,8},{25... | collective-permute-start | bytes 196616 | tf_op jit(solution)/shard_map/ppermute | solution.py:16
  23.1 2.2 %collective-permute-done.83 = bf16[16,2048]{1,0:T(8,128)(2,1)S(1)} collective-permute-done((bf16[16,2048]{1,0:T(8,128)(2,1)S(1)}, bf16[16,2048]{1,0:T(8,128)(2,1)S(1)}, u32[]{:S(2)}, u32[]{:S(2)}) %collective-permute-start.83) | collective-permute-done | bytes 65568 | tf_op jit(solution)/shard_map/ppermute | solution.py:16
  25.4 1.3 %collective-permute-start.85 = (bf16[16,2048]{1,0:T(8,128)(2,1)S(1)}, bf16[16,2048]{1,0:T(8,128)(2,1)S(1)}, u32[]{:S(2)}, u32[]{:S(2)}) collective-permute-start(bf16[16,2048]{1,0:T(8,128)(2,1)S(1)} %add.41), channel_id=1, source_target_pairs={{2,0},{3,1},{0,2},{1,3},{6,4},{7,5},{4,6},{5,7},{10,8},{11,9},{8,1... | collective-permute-start | bytes 196616 | tf_op jit(solution)/shard_map/ppermute | solution.py:16
  27.9 1.9 %collective-permute-done.86 = bf16[16,2048]{1,0:T(8,128)(2,1)S(1)} collective-permute-done((bf16[16,2048]{1,0:T(8,128)(2,1)S(1)}, bf16[16,2048]{1,0:T(8,128)(2,1)S(1)}, u32[]{:S(2)}, u32[]{:S(2)}) %collective-permute-start.86) | collective-permute-done | bytes 65568 | tf_op jit(solution)/shard_map/ppermute | solution.py:16
  30.7 40.3 %conditional.2 = (f32[64,64]{1,0:T(8,128)S(1)}, f32[256,256]{1,0:T(8,128)}, bf16[256,2048]{1,0:T(8,128)(2,1)S(1)}, f32[256,1]{1,0:T(8,128)S(1)}, bf16[256,2048]{...) conditional(s32[]{:T(128)} %bitcast.26, ...), branch_computations={%region_0.1_spmd, %region_1.2_spmd, %region_2.3_spmd, %region_3.4_... | conditional | flops 20000000000 | bytes 13631664 | solution.py:262
  31.0 5.3 %collective-permute-start.16 = (bf16[256,2048]{1,0:T(8,128)(2,1)S(1)}, bf16[256,2048]{1,0:T(8,128)(2,1)}, u32[]{:S(2)}, u32[]{:S(2)}) collective-permute-start(bf16[256,2048]{1,0:T(8,128)(2,1)S(1)} %get-tuple-element.139.own_ref), channel_id=1, source_target_pairs={{1,0},{2,1},{3,2},{4,3},{5,4},{6,5},{7,6},{8,7},{9,8},{10,9},{11,1... | collective-permute-start | bytes 3145736 | tf_op jit(solution)/shard_map/cond/branch_5_fun/ppermute | solution.py:16
  36.3 13.6 %own_tile.18 = (f32[64,64]{1,0:T(8,128)S(1)}, f32[256,256]{1,0:T(8,128)}, bf16[256,2048]{1,0:T(8,128)(2,1)S(1)}, f32[256,1]{1,0:T(8,128)S(1)}) custom-call(bf16[256,2048]{1,0:T(8,128)(2,1)S(1)} %get-tuple-element.139.own_ref, bf16[64,2048]{1,0:T(8,128)(2,1)S(1)} %get-tuple-element.140.hub_ref), custom_call_target="tpu_custom_call" | custom-call | flops 20000000000 | bytes 1048576 | tf_op jit(solution)/shard_map/cond/branch_5_fun/own_tile/pallas_call | solution.py:165
  49.8 7.2 %collective-permute-done.17 = bf16[256,2048]{1,0:T(8,128)(2,1)} collective-permute-done((bf16[256,2048]{1,0:T(8,128)(2,1)S(1)}, bf16[256,2048]{1,0:T(8,128)(2,1)}, u32[]{:S(2)}, u32[]{:S(2)}) %collective-permute-start.17) | collective-permute-done | bytes 1048608 | tf_op jit(solution)/shard_map/cond/branch_5_fun/ppermute | solution.py:16
  57.1 2.3 %collective-permute-done.16 = bf16[256,2048]{1,0:T(8,128)(2,1)} collective-permute-done((bf16[256,2048]{1,0:T(8,128)(2,1)S(1)}, bf16[256,2048]{1,0:T(8,128)(2,1)}, u32[]{:S(2)}, u32[]{:S(2)}) %collective-permute-start.16) | collective-permute-done | bytes 1048608 | tf_op jit(solution)/shard_map/cond/branch_5_fun/ppermute | solution.py:16
  59.4 11.7 %collective-permute-done.15 = bf16[256,2048]{1,0:T(8,128)(2,1)} collective-permute-done((bf16[256,2048]{1,0:T(8,128)(2,1)S(1)}, bf16[256,2048]{1,0:T(8,128)(2,1)}, u32[]{:S(2)}, u32[]{:S(2)}) %collective-permute-start.15) | collective-permute-done | bytes 1048608 | tf_op jit(solution)/shard_map/cond/branch_5_fun/ppermute | solution.py:16
  71.1 6.9 %tiles.1 = (bf16[3,256,256]{2,1,0:T(8,128)(2,1)S(1)}, bf16[3,256,256]{2,1,0:T(8,128)(2,1)S(1)}) custom-call(bf16[256,2048]{1,0:T(8,128)(2,1)} %get-tuple-element.230.far_ref, bf16[256,2048]{1,0:T(8,128)(2,1)} %get-tuple-element.231.next_ref, bf16[256,2048]{1,0:T(8,128)(2,1)S(1)} %get-tuple-element.232.own_ref, f32[256,1]{1,0:T(8,128)S(1)} %get-tuple-element.233.scale_ref, ...), custom_call_target="tpu_custom_call" | custom-call | tf_op jit(solution)/shard_map/tiles/pallas_call | solution.py:201
  78.0 12.8 %conditional.3 = (bf16[256,256]{1,0:T(8,128)(2,1)}, bf16[256,256]{1,0:T(8,128)(2,1)}, bf16[3,256,256]{2,1,0:T(8,128)(2,1)}, bf16[3,256,256]{2,1,0:T(8,128)(2,1)S(1)}, bf16[3,256,256]{2,1,0:T(8,128)(2,1)S(1)}) conditional(s32[]{:T(128)} %bitcast.26, (bf16[3,256,256]{2,1,0:T(8,128)(2,1)S(1)}, ...), branch_computations={%region_13.14_spmd, %region_14.15_spmd, %region_15.16_spmd, %regio... | conditional | bytes 3145888 | solution.py:271
  78.1 1.5 %collective-permute-start.55 = (bf16[256,256]{1,0:T(8,128)(2,1)S(1)}, bf16[256,256]{1,0:T(8,128)(2,1)}, u32[]{:S(2)}, u32[]{:S(2)}) collective-permute-start(bf16[256,256]{1,0:T(8,128)(2,1)S(1)} %get-tuple-element.252), channel_id=1, source_target_pairs={{1,0},{2,1},{3,2},{4,3},{5,4},{6,5},{7,6},{8,7},{9,8},{10,9},{11,1... | collective-permute-start | bytes 393224 | tf_op jit(solution)/shard_map/cond/branch_5_fun/ppermute | solution.py:16
  79.7 3.9 %collective-permute-done.55 = bf16[256,256]{1,0:T(8,128)(2,1)} collective-permute-done((bf16[256,256]{1,0:T(8,128)(2,1)S(1)}, bf16[256,256]{1,0:T(8,128)(2,1)}, u32[]{:S(2)}, u32[]{:S(2)}) %collective-permute-start.55) | collective-permute-done | bytes 131104 | tf_op jit(solution)/shard_map/cond/branch_5_fun/ppermute | solution.py:16
  83.6 7.2 %collective-permute-done.54 = bf16[256,256]{1,0:T(8,128)(2,1)} collective-permute-done((bf16[256,256]{1,0:T(8,128)(2,1)S(1)}, bf16[256,256]{1,0:T(8,128)(2,1)}, u32[]{:S(2)}, u32[]{:S(2)}) %collective-permute-start.54) | collective-permute-done | bytes 131104 | tf_op jit(solution)/shard_map/cond/branch_5_fun/ppermute | solution.py:16
  91.4 3.3 %stats.1 = (f32[3,256,256]{2,1,0:T(8,128)}, f32[3,256,256]{2,1,0:T(8,128)}) custom-call(bf16[256,256]{1,0:T(8,128)(2,1)} %get-tuple-element.236.next_ref, bf16[256,256]{1,0:T(8,128)(2,1)} %slice_bitcast_fusion.26.own_ref, bf16[256,256]{1,0:T(8,128)(2,1)} %get-tuple-element.238.last_ref, bf16[3,256,256]{2,1,0:T(8,128)(2,1)} %get-tuple-element.239.back_ref), custom_call_target="tpu_custom_call" | custom-call | tf_op jit(solution)/shard_map/stats/pallas_call | solution.py:219
  (30 shorter events, 4.6 us)
Async XLA Ops:
  0.6 0.7 copy-start.1
  3.6 27.1 %copy-start = (bf16[256,2048]{1,0:T(8,128)(2,1)S(1)}, bf16[256,2048]{1,0:T(8,128)(2,1)}, u32[]{:S(2)}) copy-start(bf16[256,2048]{1,0:T(8,128)(2,1)} %param.29) | copy-start | bytes 3145732
  3.6 3.2 %collective-permute-start.78 = (bf16[16,2048]{1,0:T(8,128)(2,1)S(1)}, bf16[16,2048]{1,0:T(8,128)(2,1)S(1)}, u32[]{:S(2)}, u32[]{:S(2)}) collective-permute-start(bf16[16,2048]{1,0:T(8,128)(2,1)S(1)} %get-tuple-element.268), channel_id=1, source_target_pairs={{1,0},{0,1},{3,2},{2,3},{5,4},{4,5},{7,6},{6,7},{9,8},{8,9},{11,10... | collective-permute-start | bytes 196616 | tf_op jit(solution)/shard_map/ppermute | solution.py:16
  4.2 5.1 %collective-permute-start.80 = (bf16[16,2048]{1,0:T(8,128)(2,1)S(1)}, bf16[16,2048]{1,0:T(8,128)(2,1)S(1)}, u32[]{:S(2)}, u32[]{:S(2)}) collective-permute-start(bf16[16,2048]{1,0:T(8,128)(2,1)S(1)} %get-tuple-element.269), channel_id=1, source_target_pairs={{3,0},{2,1},{1,2},{0,3},{7,4},{6,5},{5,6},{4,7},{11,8},{10,9},{9,1... | collective-permute-start | bytes 196616 | tf_op jit(solution)/shard_map/ppermute | solution.py:16
  6.8 4.3 %collective-permute-start.79 = (bf16[16,2048]{1,0:T(8,128)(2,1)S(1)}, bf16[16,2048]{1,0:T(8,128)(2,1)S(1)}, u32[]{:S(2)}, u32[]{:S(2)}) collective-permute-start(bf16[16,2048]{1,0:T(8,128)(2,1)S(1)} %get-tuple-element.270), channel_id=1, source_target_pairs={{2,0},{3,1},{0,2},{1,3},{6,4},{7,5},{4,6},{5,7},{10,8},{11,9},{8,1... | collective-permute-start | bytes 196616 | tf_op jit(solution)/shard_map/ppermute | solution.py:16
  11.1 4.3 %collective-permute-start.81 = (bf16[16,2048]{1,0:T(8,128)(2,1)S(1)}, bf16[16,2048]{1,0:T(8,128)(2,1)S(1)}, u32[]{:S(2)}, u32[]{:S(2)}) collective-permute-start(bf16[16,2048]{1,0:T(8,128)(2,1)S(1)} %fusion.1), channel_id=1, source_target_pairs={{4,0},{5,1},{6,2},{7,3},{0,4},{1,5},{2,6},{3,7},{12,8},{13,9},{14,... | collective-permute-start | bytes 196616 | tf_op jit(solution)/shard_map/ppermute | solution.py:16
  15.4 4.3 %collective-permute-start.82 = (bf16[16,2048]{1,0:T(8,128)(2,1)S(1)}, bf16[16,2048]{1,0:T(8,128)(2,1)S(1)}, u32[]{:S(2)}, u32[]{:S(2)}) collective-permute-start(bf16[16,2048]{1,0:T(8,128)(2,1)S(1)} %add.39), channel_id=1, source_target_pairs={{8,0},{9,1},{10,2},{11,3},{12,4},{13,5},{14,6},{15,7},{0,8},{1,9},... | collective-permute-start | bytes 196616 | tf_op jit(solution)/shard_map/ppermute | solution.py:16
  19.8 5.5 %collective-permute-start.83 = (bf16[16,2048]{1,0:T(8,128)(2,1)S(1)}, bf16[16,2048]{1,0:T(8,128)(2,1)S(1)}, u32[]{:S(2)}, u32[]{:S(2)}) collective-permute-start(bf16[16,2048]{1,0:T(8,128)(2,1)S(1)} %add.40), channel_id=1, source_target_pairs={{16,0},{17,1},{18,2},{19,3},{20,4},{21,5},{22,6},{23,7},{24,8},{25... | collective-permute-start | bytes 196616 | tf_op jit(solution)/shard_map/ppermute | solution.py:16
  25.3 4.5 %collective-permute-start.86 = (bf16[16,2048]{1,0:T(8,128)(2,1)S(1)}, bf16[16,2048]{1,0:T(8,128)(2,1)S(1)}, u32[]{:S(2)}, u32[]{:S(2)}) collective-permute-start(bf16[16,2048]{1,0:T(8,128)(2,1)S(1)} %add.41), channel_id=1, source_target_pairs={{3,0},{2,1},{1,2},{0,3},{7,4},{6,5},{5,6},{4,7},{11,8},{10,9},{9,1... | collective-permute-start | bytes 196616 | tf_op jit(solution)/shard_map/ppermute | solution.py:16
  25.4 5.3 %collective-permute-start.85 = (bf16[16,2048]{1,0:T(8,128)(2,1)S(1)}, bf16[16,2048]{1,0:T(8,128)(2,1)S(1)}, u32[]{:S(2)}, u32[]{:S(2)}) collective-permute-start(bf16[16,2048]{1,0:T(8,128)(2,1)S(1)} %add.41), channel_id=1, source_target_pairs={{2,0},{3,1},{0,2},{1,3},{6,4},{7,5},{4,6},{5,7},{10,8},{11,9},{8,1... | collective-permute-start | bytes 196616 | tf_op jit(solution)/shard_map/ppermute | solution.py:16
  26.7 4.0 %collective-permute-start.84 = (bf16[16,2048]{1,0:T(8,128)(2,1)S(1)}, bf16[16,2048]{1,0:T(8,128)(2,1)S(1)}, u32[]{:S(2)}, u32[]{:S(2)}) collective-permute-start(bf16[16,2048]{1,0:T(8,128)(2,1)S(1)} %add.41), channel_id=1, source_target_pairs={{1,0},{0,1},{3,2},{2,3},{5,4},{4,5},{7,6},{6,7},{9,8},{8,9},{11,10... | collective-permute-start | bytes 196616 | tf_op jit(solution)/shard_map/ppermute | solution.py:16
  30.8 26.3 %collective-permute-start.17 = (bf16[256,2048]{1,0:T(8,128)(2,1)S(1)}, bf16[256,2048]{1,0:T(8,128)(2,1)}, u32[]{:S(2)}, u32[]{:S(2)}) collective-permute-start(bf16[256,2048]{1,0:T(8,128)(2,1)S(1)} %get-tuple-element.139.own_ref), channel_id=1, source_target_pairs={{31,0},{0,1},{1,2},{2,3},{3,4},{4,5},{5,6},{6,7},{7,8},{8,9},{9,10... | collective-permute-start | bytes 3145736 | tf_op jit(solution)/shard_map/cond/branch_5_fun/ppermute | solution.py:16
  31.0 28.4 %collective-permute-start.16 = (bf16[256,2048]{1,0:T(8,128)(2,1)S(1)}, bf16[256,2048]{1,0:T(8,128)(2,1)}, u32[]{:S(2)}, u32[]{:S(2)}) collective-permute-start(bf16[256,2048]{1,0:T(8,128)(2,1)S(1)} %get-tuple-element.139.own_ref), channel_id=1, source_target_pairs={{1,0},{2,1},{3,2},{4,3},{5,4},{6,5},{7,6},{8,7},{9,8},{10,9},{11,1... | collective-permute-start | bytes 3145736 | tf_op jit(solution)/shard_map/cond/branch_5_fun/ppermute | solution.py:16
  36.3 34.8 %collective-permute-start.15 = (bf16[256,2048]{1,0:T(8,128)(2,1)S(1)}, bf16[256,2048]{1,0:T(8,128)(2,1)}, u32[]{:S(2)}, u32[]{:S(2)}) collective-permute-start(bf16[256,2048]{1,0:T(8,128)(2,1)S(1)} %get-tuple-element.139.own_ref), channel_id=1, source_target_pairs={{7,0},{8,1},{9,2},{10,3},{11,4},{12,5},{13,6},{14,7},{15,8},{16,9}... | collective-permute-start | bytes 3145736 | tf_op jit(solution)/shard_map/cond/branch_5_fun/ppermute | solution.py:16
  78.0 12.7 %collective-permute-start.56 = (bf16[3,256,256]{2,1,0:T(8,128)(2,1)S(1)}, bf16[3,256,256]{2,1,0:T(8,128)(2,1)}, u32[]{:S(2)}, u32[]{:S(2)}) collective-permute-start(bf16[3,256,256]{2,1,0:T(8,128)(2,1)S(1)} %get-tuple-element.198), channel_id=1, source_target_pairs={{25,0},{26,1},{27,2},{28,3},{29,4},{30,5},{31,6},{0,7},{1,8},{2,9}... | collective-permute-start | bytes 1179656 | tf_op jit(solution)/shard_map/cond/branch_5_fun/ppermute | solution.py:16
  78.1 5.4 %collective-permute-start.55 = (bf16[256,256]{1,0:T(8,128)(2,1)S(1)}, bf16[256,256]{1,0:T(8,128)(2,1)}, u32[]{:S(2)}, u32[]{:S(2)}) collective-permute-start(bf16[256,256]{1,0:T(8,128)(2,1)S(1)} %get-tuple-element.252), channel_id=1, source_target_pairs={{1,0},{2,1},{3,2},{4,3},{5,4},{6,5},{7,6},{8,7},{9,8},{10,9},{11,1... | collective-permute-start | bytes 393224 | tf_op jit(solution)/shard_map/cond/branch_5_fun/ppermute | solution.py:16
  79.7 11.1 %collective-permute-start.54 = (bf16[256,256]{1,0:T(8,128)(2,1)S(1)}, bf16[256,256]{1,0:T(8,128)(2,1)}, u32[]{:S(2)}, u32[]{:S(2)}) collective-permute-start(bf16[256,256]{1,0:T(8,128)(2,1)S(1)} %get-tuple-element.253), channel_id=1, source_target_pairs={{31,0},{0,1},{1,2},{2,3},{3,4},{4,5},{5,6},{6,7},{7,8},{8,9},{9,10... | collective-permute-start | bytes 393224 | tf_op jit(solution)/shard_map/cond/branch_5_fun/ppermute | solution.py:16
